TPU v7x, 32 devices: a whole 2x2x4 slice. The times are simulated.
32 devices in a mesh: io: 16 (over z, x, core), rep: 2 (over y).
Axes of the slice: x: 2, y: 2, z: 4, core: 2. Of those that a mesh axis runs over, the one named last changes fastest.
Arguments:
- snapshots: float32 [49152, 2048], P(('rep', 'io')), parts along dimension 0, may hold values from -6 to 6
Outputs:
- coefficients: float32 [32, 256, 2048], P('rep', None, 'io'), parts along dimension 0
- resid_var: float32 [512, 2048], P('rep', 'io'), parts along dimension 0
There are 2 independent parts, one for each index of `rep`. A program takes and returns all parts, laid end to end along the dimension named above; each array names one. Nothing has to cross between parts.
All inputs are finite; a program needn't handle non-finite values.
Results may differ from a plain program's by a relative error of at most 0.000071.
Values sent between devices are 32-bit elements; how exact they have to be, the bound alone decides.
A program may use at most 128 MiB of HBM per device.

v0:
```python
import jax
import jax.numpy as jnp
from jax import lax
from jax.sharding import PartitionSpec as P

TIMES = 96
HARM = 16


def basis_matrix(times):
    steps = jnp.arange(times).astype(jnp.float32)
    columns = [jnp.ones_like(steps), (steps - (times - 1) / 2.0) / (times / 2.0)]
    for harmonic in range(1, 7):
        columns.append(jnp.cos(2.0 * jnp.pi * harmonic * steps / 12.0))
    for harmonic in range(1, 6):
        columns.append(jnp.sin(2.0 * jnp.pi * harmonic * steps / 12.0))
    columns.append(jnp.cos(2.0 * jnp.pi * steps / times))
    columns.append(jnp.sin(2.0 * jnp.pi * steps / times))
    columns.append(jnp.cos(4.0 * jnp.pi * steps / times))
    return jnp.stack(columns, axis=1)


def projector_of(basis):
    gram = jnp.dot(basis.T, basis, precision=lax.Precision.HIGHEST)
    factor = jnp.linalg.cholesky(gram)
    middle = lax.linalg.triangular_solve(factor, basis.T, left_side=True, lower=True)
    return lax.linalg.triangular_solve(factor, middle, left_side=True, lower=True, transpose_a=True)


def fit_block(block, basis, projector):
    width = block.shape[-1]
    lat_rows = block.shape[0] // TIMES
    series = block.reshape(TIMES, lat_rows * width)
    coeffs = jnp.dot(projector, series, precision=lax.Precision.HIGHEST)
    moments = jnp.dot(basis.T, series, precision=lax.Precision.HIGHEST)
    total = jnp.sum(series * series, axis=0)
    variance = (total - jnp.sum(coeffs * moments, axis=0)) / TIMES
    return (coeffs.reshape(HARM, lat_rows, width), variance.reshape(1, lat_rows, width))


def local(snapshots):
    groups = lax.axis_size("io")
    local_rows = snapshots.shape[0]
    lon_dev = snapshots.shape[1] // groups
    split_view = snapshots.reshape(local_rows, groups, lon_dev)
    basis = basis_matrix(TIMES)
    projector = projector_of(basis)
    moved = lax.all_to_all(split_view, "io", split_axis=1, concat_axis=0, tiled=True)
    coeffs, variance = fit_block(moved[:, 0, :], basis, projector)
    return (coeffs, variance[0])


def solution(mesh):
    placed = (P(("rep", "io"), None),)
    return jax.shard_map(
        local,
        mesh=mesh,
        in_specs=placed,
        out_specs=(P("rep", None, "io"), P("rep", "io")),
        check_vma=False,
    )
```

profile of v0, /device:TPU:11, one launch (start us, length us, event | category | flops | bytes accessed | tf_op | source)
XLA Modules:
  0.0 326.1 jit_solution(2681641074615959106)
XLA Ops:
  0.6 10.3 %copy_bitcast_fusion = f32[1536,16,128]{2,0,1:T(8,128)} fusion(f32[1536,2048]{1,0:T(8,128)} %param.1), kind=kLoop, calls=%fused_computation.1 | loop fusion | bytes 25165824 | tf_op jit(solution)/shard_map/reshape | solution.py:45
  10.9 6.5 %all-to-all-start = ((f32[1536,16,128]{2,0,1:T(8,128)}), f32[1536,16,128]{2,0,1:T(8,128)}, u32[]{:S(2)}, u32[]{:S(2)}) async-start(f32[1536,16,128]{2,0,1:T(8,128)} %copy_bitcast_fusion), calls=%async_computation | async-start | bytes 25165824 | tf_op jit(solution)/shard_map/all_to_all | solution.py:48
  17.5 0.1 fusion.16
  17.6 0.1 fusion.14
  17.6 0.1 fusion.12
  17.7 0.1 fusion.10
  17.7 0.1 fusion.8
  17.8 0.1 multiply_cosine_fusion
  17.9 0.1 stack.2
  18.0 0.1 fusion.19
  18.1 0.1 copy.6
  18.2 1.5 cholesky.16
  19.7 0.6 compare_reduce_fusion
  20.3 0.6 fusion.1
  21.0 1.2 custom-call.8
  22.2 0.2 fusion.4
  22.4 0.1 fusion.2
  22.5 267.2 %all-to-all-done = f32[1536,16,128]{2,0,1:T(8,128)} async-done(((f32[1536,16,128]{2,0,1:T(8,128)}), f32[1536,16,128]{2,0,1:T(8,128)}, u32[]{:S(2)}, u32[]{:S(2)}) %all-to-all-start) | async-done | bytes 12582944 | tf_op jit(solution)/shard_map/all_to_all | solution.py:48
  289.7 13.8 %reshape_squeeze.3 = f32[96,32768]{1,0:T(8,128)} reshape(f32[16,1536,1,128]{3,1,0,2:T(8,128)} %bitcast.4) | data formatting | bytes 25165824 | tf_op jit(solution)/shard_map/reshape;squeeze | solution.py:33
  303.5 0.0 copy-start
  303.5 5.8 %multiply_reduce_fusion = f32[32768]{0:T(1024)S(1)} fusion(f32[96,32768]{1,0:T(8,128)} %reshape_squeeze.3), kind=kLoop, calls=%fused_computation.2 | loop fusion | flops 6258688 | bytes 12713984 | tf_op jit(solution)/shard_map/reduce_sum | solution.py:36
  309.3 2.4 copy-done
  311.7 6.0 %fusion.20 = f32[16,32768]{1,0:T(8,128)S(1)} fusion(f32[16,96]{1,0:T(8,128)S(1)} %fusion.2, f32[96,32768]{1,0:T(8,128)S(1)} %copy-done), kind=kOutput, calls=%fused_computation.39 | convolution fusion | flops 603979776 | bytes 14686208 | tf_op jit(solution)/shard_map/dot_general | solution.py:34
  317.6 6.1 %fusion = f32[32768]{0:T(1024)S(1)} fusion(f32[16,32768]{1,0:T(8,128)S(1)} %fusion.20, f32[96,16]{0,1:T(8,128)S(1)} %stack.2, f32[96,32768]{1,0:T(8,128)S(1)} %copy-done), kind=kOutput, calls=%fused_computation.3 | convolution fusion | flops 604995584 | bytes 14817280 | tf_op jit(solution)/shard_map/dot_general | solution.py:35
  323.7 1.7 copy.9
  325.4 0.7 multiply_bitcast_fusion
  (5 shorter events, 0.1 us)
Async XLA Ops:
  10.9 278.8 %all-to-all-start = ((f32[1536,16,128]{2,0,1:T(8,128)}), f32[1536,16,128]{2,0,1:T(8,128)}, u32[]{:S(2)}, u32[]{:S(2)}) async-start(f32[1536,16,128]{2,0,1:T(8,128)} %copy_bitcast_fusion), calls=%async_computation | async-start | bytes 25165824 | tf_op jit(solution)/shard_map/all_to_all | solution.py:48
  303.5 8.2 %copy-start = (f32[96,32768]{1,0:T(8,128)S(1)}, f32[96,32768]{1,0:T(8,128)}, u32[]{:S(2)}) copy-start(f32[96,32768]{1,0:T(8,128)} %reshape_squeeze.3) | copy-start | bytes 37748740
where the time goes:
time: 327 us; the launch traced here: 326 us
  waiting for transfers between devices  267 us (82%)
  local copies, waits for them, and re-layouts  28.3 us (9%)
  matrix products  12.5 us (4%)
  other arithmetic  10.9 us (3%)
  starting transfers between devices  6.52 us (2%)
    all_to_all x1, waiting for transfers between devices, local(): lax.all_to_all(split_view, 'io', split_axis=1, concat_axis=0, tiled=True)  267 us
    another operation x1, local copies, waits for them, and re-layouts, fit_block(): series = block.reshape(TIMES, lat_rows * width)  13.8 us
    reshape x1, local copies, waits for them, and re-layouts, local(): split_view = snapshots.reshape(local_rows, groups, lon_dev)  10.3 us
  transfers between devices with their start and end apart: 1, of which 1 were waited for; matrix products, arithmetic and copies ran while one was open for 2% of the time, Pallas kernels for 0%

commit v1 on v0

--- a/solution.py
+++ b/solution.py
@@ -45,7 +45,10 @@
     split_view = snapshots.reshape(local_rows, groups, lon_dev)
     basis = basis_matrix(TIMES)
     projector = projector_of(basis)
-    moved = lax.all_to_all(split_view, "io", split_axis=1, concat_axis=0, tiled=True)
+    size = lax.axis_size("io")
+    shards = jnp.stack(jnp.split(split_view, size, axis=1), axis=0)
+    shards = lax.all_to_all(shards, "io", split_axis=0, concat_axis=0)
+    moved = jnp.concatenate(shards, axis=0)
     coeffs, variance = fit_block(moved[:, 0, :], basis, projector)
     return (coeffs, variance[0])
 

time: 327 us -> 392 us (1.20)
  local copies, waits for them, and re-layouts: 28.3 us -> 93.7 us
    split x0 -> x1, local copies, waits for them, and re-layouts: none -> 39.1 us  [local(): shards = jnp.stack(jnp.split(split_view, size, axis=1), axis=0)]
    unnamed x3 -> x27, local copies, waits for them, and re-layouts: 4.09 us -> 39.7 us
    reshape x1 -> x0, local copies, waits for them, and re-layouts: 10.3 us -> none  [local(): split_view = snapshots.reshape(local_rows, groups, lon_dev)]
  transfers between devices with their start and end apart: 1 -> 1, of which waited for: 1 -> 1; matrix products, arithmetic and copies ran while one was open for 2% -> 1% of each run, Pallas kernels for 0% -> 0%
where the time goes in v1:
time: 392 us
  waiting for transfers between devices  267 us (68%)
  local copies, waits for them, and re-layouts  93.7 us (24%)
  matrix products  12.5 us (3%)
  other arithmetic  10.9 us (3%)
  starting transfers between devices  6.52 us (2%)
    all_to_all x1, waiting for transfers between devices, local(): shards = lax.all_to_all(shards, 'io', split_axis=0, concat_axis=0)  267 us
    unnamed x27, local copies, waits for them, and re-layouts  39.7 us
    split x1, local copies, waits for them, and re-layouts, local(): shards = jnp.stack(jnp.split(split_view, size, axis=1), axis=0)  39.1 us
    another operation x1, local copies, waits for them, and re-layouts, fit_block(): series = block.reshape(TIMES, lat_rows * width)  13.8 us
  transfers between devices with their start and end apart: 1, of which 1 were waited for; matrix products, arithmetic and copies ran while one was open for 1% of the time, Pallas kernels for 0%

profile of v1, /device:TPU:11, one launch (start us, length us, event | category | flops | bytes accessed | tf_op | source)
XLA Modules:
  0.0 391.5 jit_solution(15239439849811728294)
XLA Ops:
  0.6 12.2 %copy.50 = f32[192,8,16,128]{3,2,1,0:T(8,128)} copy(f32[192,8,16,128]{3,1,2,0:T(8,128)} %bitcast.77) | data formatting | bytes 25165824
  12.8 39.1 %fusion.19 = (f32[1536,1,128]{2,1,0:T(1,128)S(1)}, f32[1536,1,128]{2,1,0:T(1,128)S(1)}, f32[1536,1,128]{2,1,0:T(1,128)S(1)}, f32[1536,1,128]{2,1,0:T(1,128)}, f3...) fusion(f32[1536,16,128]{2,1,0:T(8,128)} %bitcast.75), kind=kLoop, calls=%fused_computation.53 | loop fusion | bytes 25165824 | tf_op jit(solution)/shard_map/split | solution.py:49
  52.0 2.2 constant_dynamic-update-slice_fusion.15
  54.2 2.1 constant_dynamic-update-slice_fusion.14
  56.3 2.1 constant_dynamic-update-slice_fusion.13
  58.3 2.1 constant_dynamic-update-slice_fusion.12
  60.4 2.1 constant_dynamic-update-slice_fusion.11
  62.5 2.1 constant_dynamic-update-slice_fusion.10
  64.5 2.1 constant_dynamic-update-slice_fusion.9
  66.6 2.1 constant_dynamic-update-slice_fusion.8
  68.7 0.9 constant_dynamic-update-slice_fusion.7
  69.6 0.9 constant_dynamic-update-slice_fusion.6
  70.6 1.0 constant_dynamic-update-slice_fusion.5
  71.6 1.0 constant_dynamic-update-slice_fusion.4
  72.6 0.9 constant_dynamic-update-slice_fusion.3
  73.5 1.0 constant_dynamic-update-slice_fusion.2
  74.5 0.9 constant_dynamic-update-slice_fusion.1
  75.4 1.0 constant_dynamic-update-slice_fusion
  76.4 6.5 %all-to-all-start = ((f32[16,1536,1,128]{3,1,2,0:T(8,128)}), f32[16,1536,1,128]{3,1,2,0:T(8,128)}, u32[]{:S(2)}, u32[]{:S(2)}) async-start(f32[16,1536,1,128]{3,1,2,0:T(8,128)} %constant_dynamic-update-slice_fusion), calls=%async_computation | async-start | bytes 25165824 | tf_op jit(solution)/shard_map/all_to_all | solution.py:50
  83.6 1.5 cholesky.16
  85.1 0.6 compare_reduce_fusion
  85.7 0.6 fusion.1
  86.4 1.2 custom-call.8
  87.6 0.2 fusion.4
  88.0 267.2 %all-to-all-done = f32[16,1536,1,128]{3,1,2,0:T(8,128)} async-done(((f32[16,1536,1,128]{3,1,2,0:T(8,128)}), f32[16,1536,1,128]{3,1,2,0:T(8,128)}, u32[]{:S(2)}, u32[]{:S(2)}) %all-to-all-start) | async-done | bytes 12582944 | tf_op jit(solution)/shard_map/all_to_all | solution.py:50
  355.1 13.8 %reshape_squeeze_reshape.3 = f32[96,32768]{1,0:T(8,128)} reshape(f32[16,1536,1,128]{3,1,2,0:T(8,128)} %all-to-all-done) | data formatting | bytes 25165824 | tf_op jit(solution)/shard_map/reshape;squeeze;reshape | solution.py:33
  368.9 5.8 %multiply_reduce_fusion = f32[32768]{0:T(1024)S(1)} fusion(f32[96,32768]{1,0:T(8,128)} %reshape_squeeze_reshape.3), kind=kLoop, calls=%fused_computation.1 | loop fusion | flops 6258688 | bytes 12713984 | tf_op jit(solution)/shard_map/reduce_sum | solution.py:36
  374.7 2.4 copy-done
  377.1 6.0 %fusion.21 = f32[16,32768]{1,0:T(8,128)S(1)} fusion(f32[16,96]{1,0:T(8,128)S(1)} %fusion.2, f32[96,32768]{1,0:T(8,128)S(1)} %copy-done), kind=kOutput, calls=%fused_computation.55 | convolution fusion | flops 603979776 | bytes 14686208 | tf_op jit(solution)/shard_map/dot_general | solution.py:34
  383.0 6.1 %fusion = f32[32768]{0:T(1024)S(1)} fusion(f32[16,32768]{1,0:T(8,128)S(1)} %fusion.21, f32[96,16]{0,1:T(8,128)S(1)} %stack.69, f32[96,32768]{1,0:T(8,128)S(1)} %copy-done), kind=kOutput, calls=%fused_computation.2 | convolution fusion | flops 604995584 | bytes 14817280 | tf_op jit(solution)/shard_map/dot_general | solution.py:35
  389.1 1.7 copy.51
  390.8 0.7 multiply_bitcast_fusion
  (24 shorter events, 0.9 us)
Async XLA Ops:
  51.9 16.8 %copy-start.4 = (f32[1536,1,128]{2,1,0:T(1,128)S(1)}, f32[1536,1,128]{2,1,0:T(1,128)}, u32[]{:S(2)}) copy-start(f32[1536,1,128]{2,1,0:T(1,128)} %get-tuple-element.8) | copy-start | bytes 2359300
  51.9 17.7 %copy-start.3 = (f32[1536,1,128]{2,1,0:T(1,128)S(1)}, f32[1536,1,128]{2,1,0:T(1,128)}, u32[]{:S(2)}) copy-start(f32[1536,1,128]{2,1,0:T(1,128)} %get-tuple-element.7) | copy-start | bytes 2359300
  51.9 18.6 %copy-start.2 = (f32[1536,1,128]{2,1,0:T(1,128)S(1)}, f32[1536,1,128]{2,1,0:T(1,128)}, u32[]{:S(2)}) copy-start(f32[1536,1,128]{2,1,0:T(1,128)} %get-tuple-element.6) | copy-start | bytes 2359300
  51.9 19.6 %copy-start.1 = (f32[1536,1,128]{2,1,0:T(1,128)S(1)}, f32[1536,1,128]{2,1,0:T(1,128)}, u32[]{:S(2)}) copy-start(f32[1536,1,128]{2,1,0:T(1,128)} %get-tuple-element.5) | copy-start | bytes 2359300
  76.4 278.8 %all-to-all-start = ((f32[16,1536,1,128]{3,1,2,0:T(8,128)}), f32[16,1536,1,128]{3,1,2,0:T(8,128)}, u32[]{:S(2)}, u32[]{:S(2)}) async-start(f32[16,1536,1,128]{3,1,2,0:T(8,128)} %constant_dynamic-update-slice_fusion), calls=%async_computation | async-start | bytes 25165824 | tf_op jit(solution)/shard_map/all_to_all | solution.py:50
  368.9 8.2 %copy-start = (f32[96,32768]{1,0:T(8,128)S(1)}, f32[96,32768]{1,0:T(8,128)}, u32[]{:S(2)}) copy-start(f32[96,32768]{1,0:T(8,128)} %reshape_squeeze_reshape.3) | copy-start | bytes 37748740
